TPU v7x, 32 devices: a whole 2x2x4 slice. The times are simulated.
32 devices in a mesh: basin: 4 (over z), reach: 8 (over y, x, core).
Axes of the slice: x: 2, y: 2, z: 4, core: 2. Of those that a mesh axis runs over, the one named last changes fastest.
Arguments:
- sensitivity: float32 [16, 128, 256], P(None, ('basin', 'reach')), may hold values from -6 to 6
- inverse: float32 [128, 256, 256], P(('basin', 'reach')), may hold values from -0.375 to 0.375
- spread: float32 [128, 256], P(('basin', 'reach')), may hold values from -3 to 3
- gather_weight: float32 [128, 256], P(('basin', 'reach')), may hold values from -0.0625 to 0.0625
- retain: float32 [128], P(('basin', 'reach')), may hold values from 0.984375 to 1
- storage: float32 [128, 256], P(('basin', 'reach')), may hold values from 0.2 to 0.6
- conf_source: int32 [32, 8, 64], P(('basin', 'reach')), may hold values from 0 to 1023
- conf_target: int32 [32, 8, 64], P(('basin', 'reach')), may hold values from 0 to 1023
- conf_weight: float32 [32, 8, 64], P(('basin', 'reach')), may hold values from 0.1 to 0.4
Outputs:
- adjoint: float32 [16, 128, 256], P(None, ('basin', 'reach'))
All inputs are finite; a program needn't handle non-finite values.
Results may differ from a plain program's by a relative error of at most 0.00019.
Values sent between devices are 32-bit elements; how exact they have to be, the bound alone decides.
No kernel may reach another device: no remote copies, remote signals or barrier semaphores. Data moves between devices by JAX's collectives and lax.ppermute only.
A program may use at most 64 MiB of HBM per device.

v0:
```python
import jax
import jax.numpy as jnp
from jax import lax
from jax.sharding import PartitionSpec as P


def entering_2(value, axis, join, neutral):
    count, mine = (lax.axis_size(axis), lax.axis_index(axis))
    pieces = jax.tree.map(lambda part: lax.all_gather(part, axis), value)
    pieces = jax.tree.map(lambda part: part[::-1], pieces)
    mine = count - 1 - mine
    running = jax.tree.map(
        lambda part, zero: jnp.full_like(part, 0) + jnp.asarray(zero, part.dtype), value, neutral
    )

    def turn(position, running):
        longer = join(running, jax.tree.map(lambda part: part[position], pieces))
        return jax.tree.map(lambda new, old: jnp.where(position < mine, new, old), longer, running)

    return lax.fori_loop(0, count - 1, turn, running)


def from_root(value, axis, source):
    kept = jnp.where(lax.axis_index(axis) == source, value, 0).astype(value.dtype)
    return lax.psum(kept, axis)


def compose(earlier, later):
    return (later[0] * earlier[0], later[0] * earlier[1] + later[1])


def on_device(
    sensitivity,
    inverse,
    spread,
    gather_weight,
    retain,
    storage,
    conf_source,
    conf_target,
    conf_weight,
):
    blocks, reaches = spread.shape
    rows = blocks * reaches
    sources = conf_source[0]
    targets = conf_target[0].reshape(-1)
    weights = conf_weight[0]
    identity = (jnp.ones((), jnp.float32), jnp.zeros((), jnp.float32))

    def step(later, forcing_now):
        flat = later.reshape(rows)
        everyone = lax.all_gather(flat[None], "reach", axis=0, tiled=True)
        values = jnp.take_along_axis(everyone, sources, axis=1)
        fan = jnp.zeros((rows,), jnp.float32).at[targets].add((values * weights).reshape(-1))
        forcing = forcing_now + storage * later + fan.reshape(blocks, reaches)
        local = jnp.einsum("bij,bi->bj", inverse, forcing, precision=lax.Precision.HIGHEST)
        feed = jnp.sum(gather_weight * local, axis=1)
        slope = jnp.ones((), jnp.float32)
        offset = jnp.zeros((), jnp.float32)
        for block in reversed(range(blocks)):
            offset = retain[block] * offset + feed[block]
            slope = retain[block] * slope
        within = entering_2((slope, offset), "reach", compose, identity)
        inclusive = jnp.stack(compose(within, (slope, offset)))
        total = from_root(inclusive, "reach", 0)
        outer = entering_2((total[0], total[1]), "basin", compose, identity)
        prior = compose(outer, within)
        stem = prior[1]
        entering = []
        for block in reversed(range(blocks)):
            entering.append(stem)
            stem = retain[block] * stem + feed[block]
        stem_next = jnp.stack(entering[::-1])
        adjoint = local + spread * stem_next[:, None]
        return (adjoint, adjoint)

    _, adjoint = lax.scan(
        step, jnp.zeros((blocks, reaches), jnp.float32), sensitivity, reverse=True
    )
    return adjoint


def solution(mesh):
    placed = (
        P(None, ("basin", "reach"), None),
        P(("basin", "reach"), None, None),
        P(("basin", "reach"), None),
        P(("basin", "reach"), None),
        P(("basin", "reach")),
        P(("basin", "reach"), None),
        P(("basin", "reach"), None, None),
        P(("basin", "reach"), None, None),
        P(("basin", "reach"), None, None),
    )
    return jax.shard_map(
        on_device,
        mesh=mesh,
        in_specs=placed,
        out_specs=P(None, ("basin", "reach"), None),
        check_vma=False,
    )
```

profile of v0, /device:TPU:0, one launch (start us, length us, event | category | flops | bytes accessed | tf_op | source)
XLA Modules:
  0.0 1536.1 jit_solution(8450838027662102427)
XLA Ops:
  6.7 1528.7 %while.84 = (s32[]{:T(128)}, f32[4,256]{1,0:T(4,128)S(1)}, f32[16,4,256]{2,1,0:T(4,128)S(1)}, f32[16,4,256]{2,1,0:T(4,128)}, f32[4,256]{1,0:T(4,128)S(1)}, /*ind...) while((s32[]{:T(128)}, f32[4,256]{1,0:T(4,128)S(1)}, ...), condition=%wide.wide.region_8.9_spmd.clone, body=%wide.wide.region_0.8_spmd.clone.sunk | while | flops 3165268 | bytes 5459241 | solution.py:77
  34.4 13.2 all-reduce.14
  47.8 20.3 %while.85 = (s32[]{:T(128)}, f32[]{:T(128)}, f32[]{:T(128)}, s32[]{:T(128)}, f32[8]{0:T(128)S(1)}, /*index=5*/f32[8]{0:T(128)S(1)}, s32[]{:T(128)}) while((s32[]{:T(128)}, f32[]{:T(128)}, f32[]{:T(128)}, s32[]{:T(128)}, f32[8]{0:T(128)S(1)}, /*index=5*/f32[8]{0:T(128)S(1)}, s32[]{:T(128)}) %tuple.131), condition=%wide.region_4.4_spmd, body=%wide.region_3.3_spmd.sunk | while | flops 8 | bytes 172 | solution.py:20
  132.8 13.2 all-reduce.14
  146.2 20.3 %while.85 = (s32[]{:T(128)}, f32[]{:T(128)}, f32[]{:T(128)}, s32[]{:T(128)}, f32[8]{0:T(128)S(1)}, /*index=5*/f32[8]{0:T(128)S(1)}, s32[]{:T(128)}) while((s32[]{:T(128)}, f32[]{:T(128)}, f32[]{:T(128)}, s32[]{:T(128)}, f32[8]{0:T(128)S(1)}, /*index=5*/f32[8]{0:T(128)S(1)}, s32[]{:T(128)}) %tuple.131), condition=%wide.region_4.4_spmd, body=%wide.region_3.3_spmd.sunk | while | flops 8 | bytes 172 | solution.py:20
  226.6 13.2 all-reduce.14
  240.0 20.3 %while.85 = (s32[]{:T(128)}, f32[]{:T(128)}, f32[]{:T(128)}, s32[]{:T(128)}, f32[8]{0:T(128)S(1)}, /*index=5*/f32[8]{0:T(128)S(1)}, s32[]{:T(128)}) while((s32[]{:T(128)}, f32[]{:T(128)}, f32[]{:T(128)}, s32[]{:T(128)}, f32[8]{0:T(128)S(1)}, /*index=5*/f32[8]{0:T(128)S(1)}, s32[]{:T(128)}) %tuple.131), condition=%wide.region_4.4_spmd, body=%wide.region_3.3_spmd.sunk | while | flops 8 | bytes 172 | solution.py:20
  323.4 13.2 all-reduce.14
  336.8 20.3 %while.85 = (s32[]{:T(128)}, f32[]{:T(128)}, f32[]{:T(128)}, s32[]{:T(128)}, f32[8]{0:T(128)S(1)}, /*index=5*/f32[8]{0:T(128)S(1)}, s32[]{:T(128)}) while((s32[]{:T(128)}, f32[]{:T(128)}, f32[]{:T(128)}, s32[]{:T(128)}, f32[8]{0:T(128)S(1)}, /*index=5*/f32[8]{0:T(128)S(1)}, s32[]{:T(128)}) %tuple.131), condition=%wide.region_4.4_spmd, body=%wide.region_3.3_spmd.sunk | while | flops 8 | bytes 172 | solution.py:20
  417.2 13.2 all-reduce.14
  430.6 20.3 %while.85 = (s32[]{:T(128)}, f32[]{:T(128)}, f32[]{:T(128)}, s32[]{:T(128)}, f32[8]{0:T(128)S(1)}, /*index=5*/f32[8]{0:T(128)S(1)}, s32[]{:T(128)}) while((s32[]{:T(128)}, f32[]{:T(128)}, f32[]{:T(128)}, s32[]{:T(128)}, f32[8]{0:T(128)S(1)}, /*index=5*/f32[8]{0:T(128)S(1)}, s32[]{:T(128)}) %tuple.131), condition=%wide.region_4.4_spmd, body=%wide.region_3.3_spmd.sunk | while | flops 8 | bytes 172 | solution.py:20
  514.0 13.2 all-reduce.14
  527.4 20.3 %while.85 = (s32[]{:T(128)}, f32[]{:T(128)}, f32[]{:T(128)}, s32[]{:T(128)}, f32[8]{0:T(128)S(1)}, /*index=5*/f32[8]{0:T(128)S(1)}, s32[]{:T(128)}) while((s32[]{:T(128)}, f32[]{:T(128)}, f32[]{:T(128)}, s32[]{:T(128)}, f32[8]{0:T(128)S(1)}, /*index=5*/f32[8]{0:T(128)S(1)}, s32[]{:T(128)}) %tuple.131), condition=%wide.region_4.4_spmd, body=%wide.region_3.3_spmd.sunk | while | flops 8 | bytes 172 | solution.py:20
  607.8 13.2 all-reduce.14
  621.2 20.3 %while.85 = (s32[]{:T(128)}, f32[]{:T(128)}, f32[]{:T(128)}, s32[]{:T(128)}, f32[8]{0:T(128)S(1)}, /*index=5*/f32[8]{0:T(128)S(1)}, s32[]{:T(128)}) while((s32[]{:T(128)}, f32[]{:T(128)}, f32[]{:T(128)}, s32[]{:T(128)}, f32[8]{0:T(128)S(1)}, /*index=5*/f32[8]{0:T(128)S(1)}, s32[]{:T(128)}) %tuple.131), condition=%wide.region_4.4_spmd, body=%wide.region_3.3_spmd.sunk | while | flops 8 | bytes 172 | solution.py:20
  717.9 20.3 %while.85 = (s32[]{:T(128)}, f32[]{:T(128)}, f32[]{:T(128)}, s32[]{:T(128)}, f32[8]{0:T(128)S(1)}, /*index=5*/f32[8]{0:T(128)S(1)}, s32[]{:T(128)}) while((s32[]{:T(128)}, f32[]{:T(128)}, f32[]{:T(128)}, s32[]{:T(128)}, f32[8]{0:T(128)S(1)}, /*index=5*/f32[8]{0:T(128)S(1)}, s32[]{:T(128)}) %tuple.131), condition=%wide.region_4.4_spmd, body=%wide.region_3.3_spmd.sunk | while | flops 8 | bytes 172 | solution.py:20
  811.7 20.3 %while.85 = (s32[]{:T(128)}, f32[]{:T(128)}, f32[]{:T(128)}, s32[]{:T(128)}, f32[8]{0:T(128)S(1)}, /*index=5*/f32[8]{0:T(128)S(1)}, s32[]{:T(128)}) while((s32[]{:T(128)}, f32[]{:T(128)}, f32[]{:T(128)}, s32[]{:T(128)}, f32[8]{0:T(128)S(1)}, /*index=5*/f32[8]{0:T(128)S(1)}, s32[]{:T(128)}) %tuple.131), condition=%wide.region_4.4_spmd, body=%wide.region_3.3_spmd.sunk | while | flops 8 | bytes 172 | solution.py:20
  908.5 20.3 %while.85 = (s32[]{:T(128)}, f32[]{:T(128)}, f32[]{:T(128)}, s32[]{:T(128)}, f32[8]{0:T(128)S(1)}, /*index=5*/f32[8]{0:T(128)S(1)}, s32[]{:T(128)}) while((s32[]{:T(128)}, f32[]{:T(128)}, f32[]{:T(128)}, s32[]{:T(128)}, f32[8]{0:T(128)S(1)}, /*index=5*/f32[8]{0:T(128)S(1)}, s32[]{:T(128)}) %tuple.131), condition=%wide.region_4.4_spmd, body=%wide.region_3.3_spmd.sunk | while | flops 8 | bytes 172 | solution.py:20
  1002.3 20.3 %while.85 = (s32[]{:T(128)}, f32[]{:T(128)}, f32[]{:T(128)}, s32[]{:T(128)}, f32[8]{0:T(128)S(1)}, /*index=5*/f32[8]{0:T(128)S(1)}, s32[]{:T(128)}) while((s32[]{:T(128)}, f32[]{:T(128)}, f32[]{:T(128)}, s32[]{:T(128)}, f32[8]{0:T(128)S(1)}, /*index=5*/f32[8]{0:T(128)S(1)}, s32[]{:T(128)}) %tuple.131), condition=%wide.region_4.4_spmd, body=%wide.region_3.3_spmd.sunk | while | flops 8 | bytes 172 | solution.py:20
  1099.1 20.3 %while.85 = (s32[]{:T(128)}, f32[]{:T(128)}, f32[]{:T(128)}, s32[]{:T(128)}, f32[8]{0:T(128)S(1)}, /*index=5*/f32[8]{0:T(128)S(1)}, s32[]{:T(128)}) while((s32[]{:T(128)}, f32[]{:T(128)}, f32[]{:T(128)}, s32[]{:T(128)}, f32[8]{0:T(128)S(1)}, /*index=5*/f32[8]{0:T(128)S(1)}, s32[]{:T(128)}) %tuple.131), condition=%wide.region_4.4_spmd, body=%wide.region_3.3_spmd.sunk | while | flops 8 | bytes 172 | solution.py:20
  1192.9 20.3 %while.85 = (s32[]{:T(128)}, f32[]{:T(128)}, f32[]{:T(128)}, s32[]{:T(128)}, f32[8]{0:T(128)S(1)}, /*index=5*/f32[8]{0:T(128)S(1)}, s32[]{:T(128)}) while((s32[]{:T(128)}, f32[]{:T(128)}, f32[]{:T(128)}, s32[]{:T(128)}, f32[8]{0:T(128)S(1)}, /*index=5*/f32[8]{0:T(128)S(1)}, s32[]{:T(128)}) %tuple.131), condition=%wide.region_4.4_spmd, body=%wide.region_3.3_spmd.sunk | while | flops 8 | bytes 172 | solution.py:20
  1289.7 20.3 %while.85 = (s32[]{:T(128)}, f32[]{:T(128)}, f32[]{:T(128)}, s32[]{:T(128)}, f32[8]{0:T(128)S(1)}, /*index=5*/f32[8]{0:T(128)S(1)}, s32[]{:T(128)}) while((s32[]{:T(128)}, f32[]{:T(128)}, f32[]{:T(128)}, s32[]{:T(128)}, f32[8]{0:T(128)S(1)}, /*index=5*/f32[8]{0:T(128)S(1)}, s32[]{:T(128)}) %tuple.131), condition=%wide.region_4.4_spmd, body=%wide.region_3.3_spmd.sunk | while | flops 8 | bytes 172 | solution.py:20
  1383.5 20.3 %while.85 = (s32[]{:T(128)}, f32[]{:T(128)}, f32[]{:T(128)}, s32[]{:T(128)}, f32[8]{0:T(128)S(1)}, /*index=5*/f32[8]{0:T(128)S(1)}, s32[]{:T(128)}) while((s32[]{:T(128)}, f32[]{:T(128)}, f32[]{:T(128)}, s32[]{:T(128)}, f32[8]{0:T(128)S(1)}, /*index=5*/f32[8]{0:T(128)S(1)}, s32[]{:T(128)}) %tuple.131), condition=%wide.region_4.4_spmd, body=%wide.region_3.3_spmd.sunk | while | flops 8 | bytes 172 | solution.py:20
  1480.2 20.3 %while.85 = (s32[]{:T(128)}, f32[]{:T(128)}, f32[]{:T(128)}, s32[]{:T(128)}, f32[8]{0:T(128)S(1)}, /*index=5*/f32[8]{0:T(128)S(1)}, s32[]{:T(128)}) while((s32[]{:T(128)}, f32[]{:T(128)}, f32[]{:T(128)}, s32[]{:T(128)}, f32[8]{0:T(128)S(1)}, /*index=5*/f32[8]{0:T(128)S(1)}, s32[]{:T(128)}) %tuple.131), condition=%wide.region_4.4_spmd, body=%wide.region_3.3_spmd.sunk | while | flops 8 | bytes 172 | solution.py:20
  (963 shorter events, 1176.7 us)
Async XLA Ops:
  3.9 0.7 copy-start.8
  4.5 0.7 copy-start.2
  5.2 0.7 copy-start.7
  6.0 0.7 copy-start.3
  6.0 0.7 copy-start.4
  6.0 0.7 copy-start.5
  6.0 0.7 copy-start.9
  6.0 0.7 copy-start.10
  17.5 8.4 copy-start
  115.9 8.4 copy-start
  209.7 8.4 copy-start
  306.4 8.4 copy-start
  400.2 8.4 copy-start
  497.0 8.4 copy-start
  590.8 8.4 copy-start
  687.6 8.4 copy-start
  781.4 8.4 copy-start
  878.1 8.4 copy-start
  971.9 8.4 copy-start
  1068.7 8.4 copy-start
  1162.5 8.4 copy-start
  1259.3 8.4 copy-start
  1353.1 8.4 copy-start
  1449.9 8.4 copy-start
  (2 other events, 1.3 us)
where the time goes:
time: 1540 us
  blocking collectives  691 us (45%)
  loops' own time  395 us (26%)
  local copies, waits for them, and re-layouts  354 us (23%)
  other arithmetic  82.6 us (5%)
    while x32, blocking collectives  362 us
    another operation x32, loops' own time, entering_2(): return lax.fori_loop(0, count - 1, turn, running)  263 us
    dynamic_slice x320, local copies, waits for them, and re-layouts, turn(): longer = join(running, jax.tree.map(lambda part: part[position], pieces))  193 us
    psum x16, blocking collectives, from_root(): return lax.psum(kept, axis)  188 us
    all_gather x16, blocking collectives, step(): everyone = lax.all_gather(flat[None], 'reach', axis=0, tiled=True)  140 us
    another operation x1, loops' own time, on_device(): lax.scan(step, jnp.zeros((blocks, reaches), jnp.float32), sensitivity, re...  132 us
    while x224, local copies, waits for them, and re-layouts  70.9 us
    scatter-add x16, other arithmetic, step(): jnp.zeros((rows,), jnp.float32).at[targets]  65.4 us

commit v1 on v0

--- a/solution.py
+++ b/solution.py
@@ -1,7 +1,343 @@
+import functools
+
 import jax
 import jax.numpy as jnp
 from jax import lax
+from jax.experimental import pallas as pl
+from jax.experimental.pallas import tpu as pltpu
 from jax.sharding import PartitionSpec as P
+
+LANES = 128
+SUB = 8
+HIGHEST = lax.Precision.HIGHEST
+VMEM = pltpu.MemorySpace.VMEM
+SMEM = pltpu.MemorySpace.SMEM
+
+
+def vmem():
+    return pl.BlockSpec(memory_space=VMEM)
+
+
+def smem():
+    return pl.BlockSpec(memory_space=SMEM)
+
+
+def swap(value, axis, bit):
+    return lax.ppermute(value, axis, [(i, i ^ bit) for i in range(lax.axis_size(axis))])
+
+
+def prepare_kernel(inv_ref, gather_ref, sent_ref, upon_ref):
+    blocks, reaches, _ = inv_ref.shape
+    halves = reaches // LANES
+    rows = halves * halves * blocks
+    for n in range(blocks):
+        for ih in range(halves):
+            for h in range(halves):
+                row = (ih * halves + h) * blocks + n
+
+                def tile(i, carry, n=n, ih=ih, h=h, row=row):
+                    block = inv_ref[n, pl.ds(ih * LANES + i * SUB, SUB), h * LANES : (h + 1) * LANES]
+                    sent_ref[pl.ds(i * SUB * rows + row, SUB, stride=rows), :] = block
+                    return carry
+
+                lax.fori_loop(0, LANES // SUB, tile, 0, unroll=4)
+    for n in range(blocks):
+        part = lax.dot_general(
+            gather_ref[...], inv_ref[n], (((1,), (1,)), ((), ())),
+            precision=HIGHEST, preferred_element_type=jnp.float32,
+        )
+        for ih in range(halves):
+            row = ih * blocks + n
+            upon_ref[row : row + 1, :] = part[n : n + 1, ih * LANES : (ih + 1) * LANES]
+
+
+def prepare(inverse, gather_weight):
+    blocks, reaches, _ = inverse.shape
+    rows = (reaches // LANES) ** 2 * blocks
+    return pl.pallas_call(
+        prepare_kernel,
+        out_shape=(
+            jax.ShapeDtypeStruct((LANES * rows, LANES), jnp.float32),
+            jax.ShapeDtypeStruct((SUB, LANES), jnp.float32),
+        ),
+        in_specs=[vmem(), vmem()],
+        out_specs=(vmem(), vmem()),
+        name="prepare",
+    )(inverse, gather_weight)
+
+
+def tables_kernel(slots, code_sm, code_ref, next_ref, head_ref, most_ref):
+    pairs = code_ref.shape[0]
+    levels = next_ref.shape[0]
+    lane = lax.broadcasted_iota(jnp.int32, (SUB, LANES), 1)
+    within = lax.rem(lane, slots)
+    most = jnp.zeros((SUB, LANES), jnp.int32)
+    for v in range(pairs):
+        code = code_ref[v]
+        seen = jnp.zeros((SUB, LANES), jnp.int32)
+        nexts = [jnp.full((SUB, LANES), -1, jnp.int32) for _ in range(levels)]
+        for d in range(1, slots):
+            same = (pltpu.roll(code, LANES - d, 1) == code) & (within + d < slots)
+            seen = seen + jnp.where(same, 1, 0)
+            for j in range(levels):
+                if d >= 1 << j:
+                    nexts[j] = jnp.where(same & (seen == 1 << j), lane + d, nexts[j])
+        for j in range(levels):
+            next_ref[j, v] = nexts[j]
+        most = jnp.maximum(most, seen)
+    most_ref[...] = most
+
+    place = lax.broadcasted_iota(jnp.int32, (SUB, LANES), 0) * LANES + lane
+    owners, sources = head_ref.shape[0], head_ref.shape[1]
+
+    def one(i, carry):
+        first = lax.rem(i // sources, LANES // slots) * slots
+        table = jnp.full((SUB, LANES), -1, jnp.int32)
+        for f in reversed(range(slots)):
+            table = jnp.where(place == code_sm[i * slots + f], first + f, table)
+        head_ref[i // sources, lax.rem(i, sources)] = table
+        return carry
+
+    lax.fori_loop(0, owners * sources, one, 0)
+
+
+def tables(codes, code_vec, slots):
+    owners, sources, _ = codes.shape
+    levels = (slots - 1).bit_length()
+    return pl.pallas_call(
+        functools.partial(tables_kernel, slots),
+        out_shape=(
+            jax.ShapeDtypeStruct((levels,) + code_vec.shape, jnp.int32),
+            jax.ShapeDtypeStruct((owners, sources, SUB, LANES), jnp.int32),
+            jax.ShapeDtypeStruct((SUB, LANES), jnp.int32),
+        ),
+        in_specs=[smem(), vmem()],
+        out_specs=(vmem(), vmem(), vmem()),
+        name="tables",
+    )(codes.reshape(-1), code_vec)
+
+
+def pick(values, lanes):
+    return jnp.take_along_axis(values, lanes, axis=1, mode="promise_in_bounds")
+
+
+def sweep_kernel(count, steps, at, *refs):
+    pieces = refs[1 : 1 + count]
+    scal = refs[0]
+    aux, slane, srow, weight, nexts, heads, most, links, inflow, mine, theirs, inv, adj, slot, fcol = refs[1 + count :]
+    pairs = slane.shape[0]
+    levels = nexts.shape[0]
+    keep, impulse = scal[0], scal[1]
+    half = SUB // 2
+
+    def relay(m, carry):
+        z = jnp.concatenate([p[m] for p in pieces], axis=0)
+        inv[pl.ds(pl.multiple_of(m * LANES, LANES), LANES), :] = z.T
+        return carry
+
+    lax.fori_loop(0, LANES, relay, 0, unroll=4)
+    adj[...] = jnp.zeros_like(adj)
+    seen = jnp.max(most[...])
+    jumps = sum((seen >= (1 << j)).astype(jnp.int32) for j in range(levels))
+    lane = lax.broadcasted_iota(jnp.int32, (SUB, LANES), 1)
+    upper = lax.broadcasted_iota(jnp.int32, (SUB, LANES), 0) < half
+
+    def step(it, leaving):
+        t = steps - 1 - it
+        rows = [adj[pl.ds(r, count, stride=SUB), :] for r in range(SUB)]
+        vals = []
+        for v in range(pairs):
+            got = jnp.zeros((SUB, LANES), jnp.float32)
+            for r in range(SUB):
+                got = jnp.where(srow[v] == r, pick(rows[r], slane[v]), got)
+            vals.append(got * weight[v])
+
+        def jump(j, vals):
+            out = []
+            for v in range(pairs):
+                n = nexts[j, v]
+                out.append(vals[v] + jnp.where(n >= 0, pick(vals[v], n & (LANES - 1)), 0.0))
+            return tuple(out)
+
+        vals = lax.fori_loop(0, jumps, jump, tuple(vals))
+        for v in range(pairs):
+            slot[v * SUB : (v + 1) * SUB, :] = vals[v]
+        force = []
+        for k in range(count):
+            fan = jnp.zeros((SUB, LANES), jnp.float32)
+            for s in range(count):
+                row = (k * pairs // count) * SUB + s
+                table = heads[k, s]
+                got = pick(jnp.broadcast_to(slot[row : row + 1, :], (SUB, LANES)), table & (LANES - 1))
+                fan = fan + jnp.where(table >= 0, got, 0.0)
+            now = aux[k, pl.ds(pl.multiple_of(t * SUB, SUB), SUB), :] * keep
+            own = adj[k * SUB : (k + 1) * SUB, :]
+            force.append(now + aux[k, at["storage"] : at["storage"] + SUB, :] * own + fan)
+        feed = jnp.concatenate(
+            [aux[k, at["upon"] : at["upon"] + SUB, :] * force[k] for k in range(count)], axis=0
+        )
+        spread_rows = []
+        for k in range(count):
+            other = pltpu.roll(force[k], half, 0)
+            spread_rows.append(jnp.where(upper, force[k], other))
+            spread_rows.append(jnp.where(upper, other, force[k]))
+        fcol[...] = jnp.concatenate(spread_rows, axis=0).T
+        stem = jnp.dot(links[...], feed, precision=HIGHEST, preferred_element_type=jnp.float32)
+        stem = jnp.sum(stem, axis=1, keepdims=True)
+        stem = stem + inflow[...] * jnp.where(it == 0, impulse, 0.0)
+
+        acc = jnp.zeros((LANES, LANES), jnp.float32)
+        for m in range(LANES):
+            acc = acc + inv[m * LANES : (m + 1) * LANES, :] * fcol[m : m + 1, :]
+        rowed = acc.T
+        for k in range(count):
+            base = 2 * k * SUB
+            local = rowed[base : base + SUB] + rowed[base + SUB : base + 2 * SUB]
+            new = local + aux[k, at["spread"] : at["spread"] + SUB, :] * stem[k * SUB : (k + 1) * SUB]
+            adj[k * SUB : (k + 1) * SUB, :] = new
+            if k == 0:
+                mine[t] = new
+            if k == 1:
+                theirs[t] = new
+        return jnp.where(lane == t, stem[count * SUB : (count + 1) * SUB], leaving)
+
+    leaving = lax.fori_loop(0, steps, step, jnp.zeros((SUB, LANES), jnp.float32))
+    mine[steps] = leaving
+    theirs[steps] = leaving
+
+
+def sweep(at, steps, scal, pieces, aux, slane, srow, weight, nexts, heads, most, links, inflow):
+    count = len(pieces)
+    out = jax.ShapeDtypeStruct((steps + 1, SUB, LANES), jnp.float32)
+    return pl.pallas_call(
+        functools.partial(sweep_kernel, count, steps, at),
+        out_shape=(out, out),
+        in_specs=[smem()] + [vmem()] * (count + 9),
+        out_specs=(vmem(), vmem()),
+        scratch_shapes=[
+            pltpu.VMEM((LANES * LANES, LANES), jnp.float32),
+            pltpu.VMEM((count * SUB, LANES), jnp.float32),
+            pltpu.VMEM((slane.shape[0] * SUB, LANES), jnp.float32),
+            pltpu.VMEM((LANES, LANES), jnp.float32),
+        ],
+        compiler_params=pltpu.CompilerParams(vmem_limit_bytes=48 * 1024 * 1024),
+        name="sweep",
+    )(scal, *pieces, aux, slane, srow, weight, nexts, heads, most, links, inflow)
+
+
+def join_kernel(steps, blocks, scal, mine, theirs, *refs):
+    far, out = refs[:-1], refs[-1]
+    plain = scal[0] > 0.0
+    entering = jnp.zeros((SUB, LANES), jnp.float32)
+    for ref in far:
+        ahead = ref[0]
+        for d in range(steps):
+            shifted = entering if d == 0 else pltpu.roll(entering, LANES - d, 1)
+            gain = jnp.broadcast_to(ref[1][:, steps - 1 - d : steps - d], (SUB, LANES))
+            ahead = ahead + jnp.where(shifted == 0.0, 0.0, gain * shifted)
+        entering = ahead
+    enter = [jnp.broadcast_to(entering[:, t : t + 1], (SUB, LANES)) for t in range(steps)]
+    a, b = mine[...], theirs[...]
+    for t in range(steps):
+        total = jnp.where(plain, a[t], b[t])
+        for d in range(steps - t):
+            response = jnp.where(plain, b[steps - 1 - d], a[steps - 1 - d])
+            total = total + jnp.where(enter[t + d] == 0.0, 0.0, response * enter[t + d])
+        for h in range(SUB // blocks):
+            out[t, :, h * LANES : (h + 1) * LANES] = total[h * blocks : (h + 1) * blocks]
+
+
+def join(scal, mine, theirs, far, steps, blocks):
+    return pl.pallas_call(
+        functools.partial(join_kernel, steps, blocks),
+        out_shape=jax.ShapeDtypeStruct((steps, blocks, SUB // blocks * LANES), jnp.float32),
+        in_specs=[smem()] + [vmem()] * (2 + len(far)),
+        out_specs=vmem(),
+        name="join",
+    )(scal, mine, theirs, *far)
+
+
+def exchange_rows(value, me, count, axis):
+    bit = 1
+    while bit < count:
+        shape = value.shape
+        split = value.reshape(shape[:axis] + (count // (2 * bit), 2, bit) + shape[axis + 1 :])
+        other = jnp.flip(split, axis + 1).reshape(shape)
+        value = jnp.where((me & bit) != 0, other, value)
+        bit *= 2
+    return value
+
+
+def on_group(sensitivity, inverse, spread, gather_weight, retain, storage, conf_source, conf_target, conf_weight):
+    steps, blocks, reaches = sensitivity.shape
+    halves = reaches // LANES
+    slots = conf_source.shape[2]
+    count, me = lax.axis_size("reach"), lax.axis_index("reach")
+
+    def to_rows(value):
+        lead = value.shape[:-2]
+        split = value.reshape(lead + (blocks, halves, LANES))
+        return jnp.swapaxes(split, -3, -2).reshape(lead + (SUB, LANES))
+
+    sent, upon = prepare(inverse, gather_weight)
+    sent = sent.reshape(LANES, -1, LANES)
+    x, y = swap(sent, "reach", 2), swap(sent, "reach", 4)
+    near = swap(sent, "reach", 1)
+    middle = LANES // 2
+    diag = jnp.concatenate([swap(x[:middle], "reach", 4), swap(y[middle:], "reach", 2)], axis=0)
+    pieces = [sent, near, x, swap(x, "reach", 1), y, swap(y, "reach", 1), diag, swap(diag, "reach", 1)]
+
+    wide = jnp.concatenate([conf_source[0], conf_target[0]], axis=1).astype(jnp.float32)
+    last = jnp.zeros((2 * SUB, LANES), jnp.float32).at[:count, :slots].set(conf_weight[0]).at[SUB, :blocks].set(retain)
+    aux = jnp.concatenate(
+        [to_rows(sensitivity).reshape(steps * SUB, LANES), to_rows(storage), to_rows(spread), upon, wide, last], axis=0
+    )
+    at = {name: (steps + i) * SUB for i, name in enumerate(("storage", "spread", "upon", "conf", "weight", "retain"))}
+    far = jnp.stack([aux, swap(aux, "reach", 2), swap(aux, "reach", 4), swap(aux, "reach", 6)])
+    aux = jnp.stack([far, swap(far, "reach", 1)], axis=1).reshape((count,) + aux.shape)
+
+    def rows_at(name, length, first=0, width=LANES):
+        return aux[:, at[name] : at[name] + length, first : first + width]
+
+    def paired(value):
+        value = value.reshape(count * slots // LANES, LANES // slots, count, slots)
+        return jnp.swapaxes(value, 1, 2).reshape(-1, count, LANES)
+
+    def coded(index):
+        row = lax.rem(index, reaches) // LANES * blocks + index // reaches
+        return row, lax.rem(index, LANES)
+
+    conf = exchange_rows(rows_at("conf", count).astype(jnp.int32), me, count, 1)
+    source_row, source_lane = coded(paired(conf[..., :slots]))
+    target_row, target_lane = coded(conf[..., slots:])
+    target = target_row * LANES + target_lane
+    weight = paired(exchange_rows(rows_at("weight", count, 0, slots), me, count, 1))
+    nexts, heads, most = tables(target, paired(target), slots)
+
+    keep = rows_at("retain", 1, 0, blocks).reshape(-1)
+    order = ((jnp.arange(count, dtype=jnp.int32) ^ me)[:, None] * blocks + jnp.arange(blocks, dtype=jnp.int32)).reshape(-1)
+    by_row = jnp.broadcast_to(order.reshape(count, 1, blocks), (count, halves, blocks)).reshape(-1)
+    to = jnp.concatenate([by_row, jnp.full((SUB,), -1, jnp.int32)])
+    past = order[:, None, None] > to[None, :, None]
+    chain = jnp.where(past & (order[:, None, None] < by_row[None, None, :]), keep[:, None, None], 1.0)
+    links = jnp.where(by_row[None, :] > to[:, None], jnp.prod(chain, axis=0), 0.0)
+    inflow = jnp.prod(jnp.where(past, keep[:, None, None], 1.0), axis=0)
+    inflow = jnp.broadcast_to(inflow, (to.shape[0], LANES))
+
+    plain = (me & 1) == 0
+    scal = jnp.where(plain, jnp.array([1.0, 0.0], jnp.float32), jnp.array([0.0, 1.0], jnp.float32))
+    mine, theirs = sweep(
+        at, steps, scal, pieces, aux, source_lane, source_row, weight, nexts, heads, most, links, inflow
+    )
+    theirs = swap(theirs, "reach", 1)
+    leaving = jnp.stack([mine[steps], theirs[steps]])
+    leaving = jnp.where(plain, leaving, leaving[::-1])
+    groups = lax.axis_size("basin")
+    far = [
+        lax.ppermute(leaving, "basin", [(g + d, g) for g in range(groups - d)])
+        for d in reversed(range(1, groups))
+    ]
+    return join(scal, mine, theirs, far, steps, blocks)
 
 
 def entering_2(value, axis, join, neutral):
@@ -80,6 +416,21 @@
     return adjoint
 
 
+def fits(args, mesh):
+    steps, blocks, reaches = args[0].shape
+    slots, count = args[6].shape[2], mesh.shape["reach"]
+    halves = reaches // LANES
+    return (
+        reaches % LANES == 0
+        and blocks * halves == SUB
+        and count == SUB
+        and count * halves * SUB == LANES
+        and LANES % slots == 0
+        and slots * 2 == LANES
+        and steps <= LANES
+    )
+
+
 def solution(mesh):
     placed = (
         P(None, ("basin", "reach"), None),
@@ -92,8 +443,11 @@
         P(("basin", "reach"), None, None),
         P(("basin", "reach"), None, None),
     )
+    def program(*args):
+        return (on_group if fits(args, mesh) else on_device)(*args)
+
     return jax.shard_map(
-        on_device,
+        program,
         mesh=mesh,
         in_specs=placed,
         out_specs=P(None, ("basin", "reach"), None),

time: 1540 us -> 110 us (0.07)
  blocking collectives: 691 us -> 0 us
  loops' own time: 395 us -> 0 us
  local copies, waits for them, and re-layouts: 354 us -> 12.2 us
  other arithmetic: 82.6 us -> 1.23 us
  Pallas kernels: 0 us -> 40.7 us
  waiting for transfers between devices: 0 us -> 39.7 us
    another operation x33 -> x0, loops' own time: 395 us -> none  [the longest x32 263 us: entering_2(): return lax.fori_loop(0, count - 1, turn, running)]
    while x32 -> x0, blocking collectives: 362 us -> none
    dynamic_slice x320 -> x0, local copies, waits for them, and re-layouts: 193 us -> none  [turn(): longer = join(running, jax.tree.map(lambda part: part[position], pieces))]
    psum x16 -> x0, blocking collectives: 188 us -> none  [from_root(): return lax.psum(kept, axis)]
    all_gather x16 -> x0, blocking collectives: 140 us -> none  [step(): everyone = lax.all_gather(flat[None], 'reach', axis=0, tiled=True)]
    while x224 -> x0, local copies, waits for them, and re-layouts: 70.9 us -> none
    scatter-add x16 -> x0, other arithmetic: 65.4 us -> none  [step(): jnp.zeros((rows,), jnp.float32).at[targets]]
    gather x32 -> x0, local copies, waits for them, and re-layouts: 58.5 us -> none  [step(): values = jnp.take_along_axis(everyone, sources, axis=1)]
  transfers between devices with their start and end apart: 0 -> 16, of which waited for: 0 -> 10; matrix products, arithmetic and copies ran while one was open for 0% -> 6% of each run, Pallas kernels for 0% -> 6%
where the time goes in v1:
time: 110 us
  Pallas kernels  40.7 us (37%)
  waiting for transfers between devices  39.7 us (36%)
  starting transfers between devices  15.3 us (14%)
  local copies, waits for them, and re-layouts  12.2 us (11%)
  other arithmetic  1.23 us (1%)
    ppermute x13, waiting for transfers between devices, swap(): lax.ppermute(value, axis, [(i, i ^ bit) for i in range(lax.axis_size(axis...  32.4 us
    pallas_call x1, Pallas kernels, sweep(): pl.pallas_call(functools.partial(sweep_kernel, count, steps, at), out_sha...  28.5 us
    ppermute x13, starting transfers between devices, swap(): lax.ppermute(value, axis, [(i, i ^ bit) for i in range(lax.axis_size(axis...  11.5 us
    ppermute x3, waiting for transfers between devices, on_group(): lax.ppermute(leaving, 'basin', [(g + d, g) for g in range(groups - d)])  7.21 us
    pallas_call x1, Pallas kernels, tables(): pl.pallas_call(functools.partial(tables_kernel, slots), out_shape=(jax.Sh...  6.61 us
    unnamed x37, local copies, waits for them, and re-layouts  6.3 us
    ppermute x3, starting transfers between devices, on_group(): lax.ppermute(leaving, 'basin', [(g + d, g) for g in range(groups - d)])  3.87 us
    pallas_call x1, Pallas kernels, prepare(): pl.pallas_call(prepare_kernel, out_shape=(jax.ShapeDtypeStruct((LANES * r...  3.63 us
  transfers between devices with their start and end apart: 16, of which 10 were waited for; matrix products, arithmetic and copies ran while one was open for 6% of the time, Pallas kernels for 6%

profile of v1, /device:TPU:0, one launch (start us, length us, event | category | flops | bytes accessed | tf_op | source)
XLA Modules:
  0.0 109.5 jit_solution(15994434570588541563)
XLA Ops:
  1.4 0.9 reshape.317
  3.0 3.6 %prepare.1 = (f32[2048,128]{1,0:T(8,128)}, f32[8,128]{1,0:T(8,128)}) custom-call(f32[4,256,256]{2,1,0:T(8,128)} %inv_ref.1, f32[4,256]{1,0:T(4,128)} %gather_ref.1), custom_call_target="tpu_custom_call" | custom-call | tf_op jit(solution)/shard_map/prepare/pallas_call | solution.py:57
  8.2 4.0 %collective-permute-start.10 = (f32[176,128]{1,0:T(8,128)S(1)}, f32[176,128]{1,0:T(8,128)S(1)}, u32[]{:S(2)}, u32[]{:S(2)}) collective-permute-start(f32[176,128]{1,0:T(8,128)S(1)} %constant_dynamic-update-slice_fusion.2), channel_id=1, source_target_pairs={{0,6},{1,7},{2,4},{3,5},{4,2},{5,3},{6,0},{7,1},{8,14},{9,15},{10,... | collective-permute-start | bytes 270344 | tf_op jit(solution)/shard_map/ppermute | solution.py:26
  12.8 1.9 %collective-permute-start.3 = (f32[128,16,128]{2,1,0:T(8,128)}, f32[128,16,128]{2,1,0:T(8,128)}, u32[]{:S(2)}, u32[]{:S(2)}) collective-permute-start(f32[128,16,128]{2,1,0:T(8,128)} %bitcast.50), channel_id=1, source_target_pairs={{0,4},{1,5},{2,6},{3,7},{4,0},{5,1},{6,2},{7,3},{8,12},{9,13},{10,... | collective-permute-start | bytes 3145736 | tf_op jit(solution)/shard_map/ppermute | solution.py:26
  14.8 1.5 %collective-permute-start.1 = (f32[128,16,128]{2,1,0:T(8,128)}, f32[128,16,128]{2,1,0:T(8,128)S(1)}, u32[]{:S(2)}, u32[]{:S(2)}) collective-permute-start(f32[128,16,128]{2,1,0:T(8,128)} %bitcast.51), channel_id=1, source_target_pairs={{0,2},{1,3},{2,0},{3,1},{4,6},{5,7},{6,4},{7,5},{8,10},{9,11},{10,... | collective-permute-start | bytes 3145736 | tf_op jit(solution)/shard_map/ppermute | solution.py:26
  16.7 1.0 collective-permute-done.9
  18.9 1.2 %collective-permute-done.11 = f32[4,176,128]{2,1,0:T(8,128)S(1)} collective-permute-done((f32[4,176,128]{2,1,0:T(8,128)S(1)}, f32[4,176,128]{2,1,0:T(8,128)S(1)}, u32[]{:S(2)}, u32[]{:S(2)}) %collective-permute-start.11) | collective-permute-done | bytes 360480 | tf_op jit(solution)/shard_map/ppermute | solution.py:26
  20.4 19.3 %collective-permute-done.1.refs_3_ = f32[128,16,128]{2,1,0:T(8,128)S(1)} collective-permute-done((f32[128,16,128]{2,1,0:T(8,128)}, f32[128,16,128]{2,1,0:T(8,128)S(1)}, u32[]{:S(2)}, u32[]{:S(2)}) %collective-permute-start.1) | collective-permute-done | bytes 1048608 | tf_op jit(solution)/shard_map/ppermute | solution.py:26
  39.8 0.9 collective-permute-start.5
  40.7 1.1 slice.76
  41.8 1.3 %collective-permute-start.6 = (f32[64,16,128]{2,1,0:T(8,128)S(1)}, f32[64,16,128]{2,1,0:T(8,128)S(1)}, u32[]{:S(2)}, u32[]{:S(2)}) collective-permute-start(f32[64,16,128]{2,1,0:T(8,128)S(1)} %slice.76), channel_id=1, source_target_pairs={{0,2},{1,3},{2,0},{3,1},{4,6},{5,7},{6,4},{7,5},{8,10},{9,11},{10,... | collective-permute-start | bytes 1572872 | tf_op jit(solution)/shard_map/ppermute | solution.py:26
  43.7 8.9 %collective-permute-done.5 = f32[64,16,128]{2,1,0:T(8,128)S(1)} collective-permute-done((f32[64,16,128]{2,1,0:T(8,128)S(1)}, f32[64,16,128]{2,1,0:T(8,128)S(1)}, u32[]{:S(2)}, u32[]{:S(2)}) %collective-permute-start.5) | collective-permute-done | bytes 524320 | tf_op jit(solution)/shard_map/ppermute | solution.py:26
  52.6 0.8 constant_dynamic-update-slice_fusion.1
  57.2 6.6 %tables.1 = (s32[6,4,8,128]{3,2,1,0:T(8,128)}, s32[8,8,8,128]{3,2,1,0:T(8,128)}, s32[8,128]{1,0:T(8,128)}) custom-call(s32[4096]{0:T(1024)} %reshape.341.code_sm, s32[4,8,128]{2,1,0:T(8,128)} %reshape.343.code_ref), custom_call_target="tpu_custom_call" | custom-call | tf_op jit(solution)/shard_map/tables/pallas_call | solution.py:107
  64.8 0.9 copy-done.1
  65.8 28.5 %sweep.1 = (f32[17,8,128]{2,1,0:T(8,128)S(1)}, f32[17,8,128]{2,1,0:T(8,128)S(1)}) custom-call(f32[2]{0:T(128)S(1)} %broadcast_select_fusion.6.refs_0_.scal, f32[128,16,128]{2,1,0:T(8,128)S(1)} %bitcast.53, f32[128,16,128]{2,1,0:T(8,128)} %collective-permute-done.refs_2_, f32[128,16,128]{2,1,0:T(8,128)S(1)} %collective-permute-done.1.refs_3_, ...), custom_call_target="tpu_custom_call" | custom-call | tf_op jit(solution)/shard_map/sweep/pallas_call | solution.py:212
  94.9 0.9 collective-permute-done.12.theirs
  95.8 1.3 %collective-permute-start.15 = (f32[2,8,128]{2,1,0:T(8,128)S(1)}, f32[2,8,128]{2,1,0:T(8,128)S(1)}, u32[]{:S(2)}, u32[]{:S(2)}) collective-permute-start(f32[2,8,128]{2,1,0:T(8,128)S(1)} %reverse_select_fusion), channel_id=1, source_target_pairs={{8,0},{16,8},{24,16},{9,1},{17,9},{25,17},{10,2},{18,10},{26,18},{... | collective-permute-start | bytes 24584 | tf_op jit(solution)/shard_map/ppermute | solution.py:337
  97.1 1.3 %collective-permute-start.14 = (f32[2,8,128]{2,1,0:T(8,128)S(1)}, f32[2,8,128]{2,1,0:T(8,128)S(1)}, u32[]{:S(2)}, u32[]{:S(2)}) collective-permute-start(f32[2,8,128]{2,1,0:T(8,128)S(1)} %reverse_select_fusion), channel_id=1, source_target_pairs={{16,0},{24,8},{17,1},{25,9},{18,2},{26,10},{19,3},{27,11},{20,4},{... | collective-permute-start | bytes 24584 | tf_op jit(solution)/shard_map/ppermute | solution.py:337
  98.4 1.3 %collective-permute-start.13 = (f32[2,8,128]{2,1,0:T(8,128)S(1)}, f32[2,8,128]{2,1,0:T(8,128)S(1)}, u32[]{:S(2)}, u32[]{:S(2)}) collective-permute-start(f32[2,8,128]{2,1,0:T(8,128)S(1)} %reverse_select_fusion), channel_id=1, source_target_pairs={{24,0},{25,1},{26,2},{27,3},{28,4},{29,5},{30,6},{31,7}} | collective-permute-start | bytes 24584 | tf_op jit(solution)/shard_map/ppermute | solution.py:337
  99.7 1.6 %collective-permute-done.15.refs_2_ = f32[2,8,128]{2,1,0:T(8,128)S(1)} collective-permute-done((f32[2,8,128]{2,1,0:T(8,128)S(1)}, f32[2,8,128]{2,1,0:T(8,128)S(1)}, u32[]{:S(2)}, u32[]{:S(2)}) %collective-permute-start.15) | collective-permute-done | bytes 8224 | tf_op jit(solution)/shard_map/ppermute | solution.py:337
  101.3 2.2 %collective-permute-done.14.refs_1_ = f32[2,8,128]{2,1,0:T(8,128)S(1)} collective-permute-done((f32[2,8,128]{2,1,0:T(8,128)S(1)}, f32[2,8,128]{2,1,0:T(8,128)S(1)}, u32[]{:S(2)}, u32[]{:S(2)}) %collective-permute-start.14) | collective-permute-done | bytes 8224 | tf_op jit(solution)/shard_map/ppermute | solution.py:337
  103.5 3.4 %collective-permute-done.13.refs_0_ = f32[2,8,128]{2,1,0:T(8,128)S(1)} collective-permute-done((f32[2,8,128]{2,1,0:T(8,128)S(1)}, f32[2,8,128]{2,1,0:T(8,128)S(1)}, u32[]{:S(2)}, u32[]{:S(2)}) %collective-permute-start.13) | collective-permute-done | bytes 8224 | tf_op jit(solution)/shard_map/ppermute | solution.py:337
  107.5 2.0 %join.1 = f32[16,4,256]{2,1,0:T(4,128)} custom-call(f32[2]{0:T(128)} %copy-done.5, f32[17,8,128]{2,1,0:T(8,128)} %copy-done.3, f32[17,8,128]{2,1,0:T(8,128)} %copy-done.6, f32[2,8,128]{2,1,0:T(8,128)} %copy-done.9, f32[2,8,128]{2,1,0:T(8,128)} %copy-done.8, f32[2,8,128]{2,1,0:T(8,128)} %copy-done.7), custom_call_target="tpu_custom_call" | custom-call | tf_op jit(solution)/shard_map/join/pallas_call | solution.py:251
  (107 shorter events, 12.8 us)
Async XLA Ops:
  8.2 8.4 %collective-permute-start.10 = (f32[176,128]{1,0:T(8,128)S(1)}, f32[176,128]{1,0:T(8,128)S(1)}, u32[]{:S(2)}, u32[]{:S(2)}) collective-permute-start(f32[176,128]{1,0:T(8,128)S(1)} %constant_dynamic-update-slice_fusion.2), channel_id=1, source_target_pairs={{0,6},{1,7},{2,4},{3,5},{4,2},{5,3},{6,0},{7,1},{8,14},{9,15},{10,... | collective-permute-start | bytes 270344 | tf_op jit(solution)/shard_map/ppermute | solution.py:26
  12.2 5.5 %collective-permute-start.9 = (f32[176,128]{1,0:T(8,128)S(1)}, f32[176,128]{1,0:T(8,128)S(1)}, u32[]{:S(2)}, u32[]{:S(2)}) collective-permute-start(f32[176,128]{1,0:T(8,128)S(1)} %constant_dynamic-update-slice_fusion.2), channel_id=1, source_target_pairs={{0,4},{1,5},{2,6},{3,7},{4,0},{5,1},{6,2},{7,3},{8,12},{9,13},{10,... | collective-permute-start | bytes 270344 | tf_op jit(solution)/shard_map/ppermute | solution.py:26
  12.7 5.5 %collective-permute-start.8 = (f32[176,128]{1,0:T(8,128)S(1)}, f32[176,128]{1,0:T(8,128)S(1)}, u32[]{:S(2)}, u32[]{:S(2)}) collective-permute-start(f32[176,128]{1,0:T(8,128)S(1)} %constant_dynamic-update-slice_fusion.2), channel_id=1, source_target_pairs={{0,2},{1,3},{2,0},{3,1},{4,6},{5,7},{6,4},{7,5},{8,10},{9,11},{10,... | collective-permute-start | bytes 270344 | tf_op jit(solution)/shard_map/ppermute | solution.py:26
  12.8 27.9 %collective-permute-start.3 = (f32[128,16,128]{2,1,0:T(8,128)}, f32[128,16,128]{2,1,0:T(8,128)}, u32[]{:S(2)}, u32[]{:S(2)}) collective-permute-start(f32[128,16,128]{2,1,0:T(8,128)} %bitcast.50), channel_id=1, source_target_pairs={{0,4},{1,5},{2,6},{3,7},{4,0},{5,1},{6,2},{7,3},{8,12},{9,13},{10,... | collective-permute-start | bytes 3145736 | tf_op jit(solution)/shard_map/ppermute | solution.py:26
  14.8 24.9 %collective-permute-start.1 = (f32[128,16,128]{2,1,0:T(8,128)}, f32[128,16,128]{2,1,0:T(8,128)S(1)}, u32[]{:S(2)}, u32[]{:S(2)}) collective-permute-start(f32[128,16,128]{2,1,0:T(8,128)} %bitcast.51), channel_id=1, source_target_pairs={{0,2},{1,3},{2,0},{3,1},{4,6},{5,7},{6,4},{7,5},{8,10},{9,11},{10,... | collective-permute-start | bytes 3145736 | tf_op jit(solution)/shard_map/ppermute | solution.py:26
  16.6 47.4 %collective-permute-start = (f32[128,16,128]{2,1,0:T(8,128)}, f32[128,16,128]{2,1,0:T(8,128)}, u32[]{:S(2)}, u32[]{:S(2)}) collective-permute-start(f32[128,16,128]{2,1,0:T(8,128)} %bitcast.52), channel_id=1, source_target_pairs={{0,1},{1,0},{2,3},{3,2},{4,5},{5,4},{6,7},{7,6},{8,9},{9,8},{10,11... | collective-permute-start | bytes 3145736 | tf_op jit(solution)/shard_map/ppermute | solution.py:26
  18.3 1.8 %collective-permute-start.11 = (f32[4,176,128]{2,1,0:T(8,128)S(1)}, f32[4,176,128]{2,1,0:T(8,128)S(1)}, u32[]{:S(2)}, u32[]{:S(2)}) collective-permute-start(f32[4,176,128]{2,1,0:T(8,128)S(1)} %get-tuple-element.44), channel_id=1, source_target_pairs={{0,1},{1,0},{2,3},{3,2},{4,5},{5,4},{6,7},{7,6},{8,9},{9,8},{10,11... | collective-permute-start | bytes 1081352 | tf_op jit(solution)/shard_map/ppermute | solution.py:26
  18.9 45.2 %copy-start.5 = (f32[2]{0:T(128)}, f32[2]{0:T(128)S(1)}, u32[]{:S(2)}) copy-start(f32[2]{0:T(128)S(1)} %broadcast_select_fusion.6.refs_0_.scal) | copy-start | bytes 28
  39.8 12.8 %collective-permute-start.5 = (f32[64,16,128]{2,1,0:T(8,128)S(1)}, f32[64,16,128]{2,1,0:T(8,128)S(1)}, u32[]{:S(2)}, u32[]{:S(2)}) collective-permute-start(f32[64,16,128]{2,1,0:T(8,128)S(1)} %slice.75), channel_id=1, source_target_pairs={{0,4},{1,5},{2,6},{3,7},{4,0},{5,1},{6,2},{7,3},{8,12},{9,13},{10,... | collective-permute-start | bytes 1572872 | tf_op jit(solution)/shard_map/ppermute | solution.py:26
  41.8 12.3 %collective-permute-start.6 = (f32[64,16,128]{2,1,0:T(8,128)S(1)}, f32[64,16,128]{2,1,0:T(8,128)S(1)}, u32[]{:S(2)}, u32[]{:S(2)}) collective-permute-start(f32[64,16,128]{2,1,0:T(8,128)S(1)} %slice.76), channel_id=1, source_target_pairs={{0,2},{1,3},{2,0},{3,1},{4,6},{5,7},{6,4},{7,5},{8,10},{9,11},{10,... | collective-permute-start | bytes 1572872 | tf_op jit(solution)/shard_map/ppermute | solution.py:26
  43.1 20.9 %collective-permute-start.4 = (f32[128,16,128]{2,1,0:T(8,128)}, f32[128,16,128]{2,1,0:T(8,128)}, u32[]{:S(2)}, u32[]{:S(2)}) collective-permute-start(f32[128,16,128]{2,1,0:T(8,128)} %collective-permute-done.3.refs_5_), channel_id=1, source_target_pairs={{0,1},{1,0},{2,3},{3,2},{4,5},{5,4},{6,7},{7,6},{8,9},{9,8},{10,11... | collective-permute-start | bytes 3145736 | tf_op jit(solution)/shard_map/ppermute | solution.py:26
  43.2 20.9 %collective-permute-start.2 = (f32[128,16,128]{2,1,0:T(8,128)S(1)}, f32[128,16,128]{2,1,0:T(8,128)}, u32[]{:S(2)}, u32[]{:S(2)}) collective-permute-start(f32[128,16,128]{2,1,0:T(8,128)S(1)} %collective-permute-done.1.refs_3_), channel_id=1, source_target_pairs={{0,1},{1,0},{2,3},{3,2},{4,5},{5,4},{6,7},{7,6},{8,9},{9,8},{10,11... | collective-permute-start | bytes 3145736 | tf_op jit(solution)/shard_map/ppermute | solution.py:26
  53.4 10.8 %copy-start = (f32[2048,128]{1,0:T(8,128)S(1)}, f32[2048,128]{1,0:T(8,128)}, u32[]{:S(2)}) copy-start(f32[2048,128]{1,0:T(8,128)} %get-tuple-element.36) | copy-start | bytes 3145732
  54.9 9.2 %collective-permute-start.7 = (f32[128,16,128]{2,1,0:T(8,128)}, f32[128,16,128]{2,1,0:T(8,128)}, u32[]{:S(2)}, u32[]{:S(2)}) collective-permute-start(f32[128,16,128]{2,1,0:T(8,128)} %constant_dynamic-update-slice_fusion.refs_7_), channel_id=1, source_target_pairs={{0,1},{1,0},{2,3},{3,2},{4,5},{5,4},{6,7},{7,6},{8,9},{9,8},{10,11... | collective-permute-start | bytes 3145736 | tf_op jit(solution)/shard_map/ppermute | solution.py:26
  63.8 0.9 copy-start.2
  64.8 0.9 copy-start.1
  94.3 12.6 %copy-start.3 = (f32[17,8,128]{2,1,0:T(8,128)}, f32[17,8,128]{2,1,0:T(8,128)S(1)}, u32[]{:S(2)}) copy-start(f32[17,8,128]{2,1,0:T(8,128)S(1)} %get-tuple-element.41.mine) | copy-start | bytes 208900
  94.3 1.5 %collective-permute-start.12 = (f32[17,8,128]{2,1,0:T(8,128)S(1)}, f32[17,8,128]{2,1,0:T(8,128)S(1)}, u32[]{:S(2)}, u32[]{:S(2)}) collective-permute-start(f32[17,8,128]{2,1,0:T(8,128)S(1)} %get-tuple-element.42), channel_id=1, source_target_pairs={{0,1},{1,0},{2,3},{3,2},{4,5},{5,4},{6,7},{7,6},{8,9},{9,8},{10,11... | collective-permute-start | bytes 208904 | tf_op jit(solution)/shard_map/ppermute | solution.py:26
  95.8 11.1 %copy-start.6 = (f32[17,8,128]{2,1,0:T(8,128)}, f32[17,8,128]{2,1,0:T(8,128)S(1)}, u32[]{:S(2)}) copy-start(f32[17,8,128]{2,1,0:T(8,128)S(1)} %collective-permute-done.12.theirs) | copy-start | bytes 208900
  95.8 5.5 %collective-permute-start.15 = (f32[2,8,128]{2,1,0:T(8,128)S(1)}, f32[2,8,128]{2,1,0:T(8,128)S(1)}, u32[]{:S(2)}, u32[]{:S(2)}) collective-permute-start(f32[2,8,128]{2,1,0:T(8,128)S(1)} %reverse_select_fusion), channel_id=1, source_target_pairs={{8,0},{16,8},{24,16},{9,1},{17,9},{25,17},{10,2},{18,10},{26,18},{... | collective-permute-start | bytes 24584 | tf_op jit(solution)/shard_map/ppermute | solution.py:337
  97.1 6.4 %collective-permute-start.14 = (f32[2,8,128]{2,1,0:T(8,128)S(1)}, f32[2,8,128]{2,1,0:T(8,128)S(1)}, u32[]{:S(2)}, u32[]{:S(2)}) collective-permute-start(f32[2,8,128]{2,1,0:T(8,128)S(1)} %reverse_select_fusion), channel_id=1, source_target_pairs={{16,0},{24,8},{17,1},{25,9},{18,2},{26,10},{19,3},{27,11},{20,4},{... | collective-permute-start | bytes 24584 | tf_op jit(solution)/shard_map/ppermute | solution.py:337
  98.4 8.5 %collective-permute-start.13 = (f32[2,8,128]{2,1,0:T(8,128)S(1)}, f32[2,8,128]{2,1,0:T(8,128)S(1)}, u32[]{:S(2)}, u32[]{:S(2)}) collective-permute-start(f32[2,8,128]{2,1,0:T(8,128)S(1)} %reverse_select_fusion), channel_id=1, source_target_pairs={{24,0},{25,1},{26,2},{27,3},{28,4},{29,5},{30,6},{31,7}} | collective-permute-start | bytes 24584 | tf_op jit(solution)/shard_map/ppermute | solution.py:337
  101.3 5.6 %copy-start.7 = (f32[2,8,128]{2,1,0:T(8,128)}, f32[2,8,128]{2,1,0:T(8,128)S(1)}, u32[]{:S(2)}) copy-start(f32[2,8,128]{2,1,0:T(8,128)S(1)} %collective-permute-done.15.refs_2_) | copy-start | bytes 24580
  103.5 3.4 %copy-start.8 = (f32[2,8,128]{2,1,0:T(8,128)}, f32[2,8,128]{2,1,0:T(8,128)S(1)}, u32[]{:S(2)}) copy-start(f32[2,8,128]{2,1,0:T(8,128)S(1)} %collective-permute-done.14.refs_1_) | copy-start | bytes 24580
  (8 other events, 5.4 us)
